TPU v7x, 256 devices: a whole 4x4x8 slice. The times are simulated.
256 devices in a mesh: dp: 8 (over x, core), fsdp: 8 (over z), mp: 4 (over y).
Axes of the slice: x: 4, y: 4, z: 8, core: 2. Of those that a mesh axis runs over, the one named last changes fastest.
Arguments:
- gradients: bfloat16 [64, 12, 2, 256, 1024], P(('dp', 'fsdp'), None, None, None, 'mp'), may hold values from -16 to 16
- master: float32 [12, 2, 256, 1024], P(None, None, ('dp', 'fsdp'), 'mp'), may hold values from -0.375 to 0.375
- teacher: float32 [12, 2, 256, 1024], P(None, None, ('dp', 'fsdp'), 'mp'), may hold values from -0.375 to 0.375
- first_moment: float32 [12, 2, 256, 1024], P(None, None, ('dp', 'fsdp'), 'mp'), may hold values from -2.2888184e-05 to 2.2888184e-05
- second_moment: float32 [12, 2, 256, 1024], P(None, None, ('dp', 'fsdp'), 'mp'), may hold values from 0 to 1, as said below
- layer_rates: float32 [12], replicated, may hold values from 0.02 to 0.2
Outputs:
- master_new: float32 [12, 2, 256, 1024], P(None, None, ('dp', 'fsdp'), 'mp')
- teacher_new: float32 [12, 2, 256, 1024], P(None, None, ('dp', 'fsdp'), 'mp')
- first_new: float32 [12, 2, 256, 1024], P(None, None, ('dp', 'fsdp'), 'mp')
- second_new: float32 [12, 2, 256, 1024], P(None, None, ('dp', 'fsdp'), 'mp')
- student_weights: bfloat16 [12, 2, 256, 1024], P(None, None, None, 'mp')
- teacher_weights: bfloat16 [12, 2, 256, 1024], P(None, None, None, 'mp')
Inputs may be any that keep to these rules, and one draw needn't show every extreme that they name: `second_moment`: every entry is positive.
All inputs are finite; a program needn't handle non-finite values.
Results may differ from a plain program's by a relative error of at most 0.0004.
Values may be sent and summed in bfloat16 or wider, within the bound.
No kernel may reach another device: no remote copies, remote signals or barrier semaphores. Data moves between devices by JAX's collectives and lax.ppermute only.
A program may use at most 64 MiB of HBM per device.

v0:
```python
import jax
import jax.numpy as jnp
from jax import lax
from jax.sharding import Mesh
from jax.sharding import PartitionSpec as P

DP = ("dp_0", "dp_1")
DP_FSDP_MP = ("dp_0", "dp_1", "fsdp", "mp")
DP_FSDP = ("dp_0", "dp_1", "fsdp")
CLIP_NORM = 0.1
BETA_ONE = 0.9
BETA_TWO = 0.999
BIAS_ONE = 1.0 - 0.9**50 * 0.9**50
BIAS_TWO = 1.0 - 0.999**50 * 0.999**50
ADAM_EPS = 1e-08
DECAY = 0.05
EMA_KEEP = 0.95


def cut_along(x, dim, length):
    before, after = (x.shape[:dim], x.shape[dim + 1 :])
    return jnp.moveaxis(x.reshape(*before, length, -1, *after), dim, 0)


def summed_on_arrival(x, axis, dim):
    length = lax.axis_size(axis)
    pieces = lax.all_to_all(cut_along(x, dim, length), axis, 0, 0, tiled=True)
    return jnp.sum(pieces, axis=0)


def by_axis(x, axes):
    for axis in axes:
        x = lax.psum(x, axis)
    return x


def side_by_side(arrays, axis, dim, along):
    ends, at = ([], 0)
    for a in arrays[:-1]:
        at += a.shape[along]
        ends.append(at)
    both = jnp.concatenate(arrays, axis=along)
    return tuple(jnp.split(lax.all_gather(both, axis, axis=dim, tiled=True), ends, axis=along))


def shards(gradients, master, teacher, first_moment, second_moment, layer_rates):
    own_grad = gradients[0].astype(jnp.float32)
    halfway = lax.psum_scatter(own_grad, DP, scatter_dimension=2, tiled=True)
    summed = summed_on_arrival(halfway, "fsdp", 2)
    mean_grad = summed / (lax.axis_size(DP) * lax.axis_size("fsdp"))
    norm_sq = by_axis(jnp.sum(mean_grad * mean_grad), DP_FSDP_MP)
    clip_factor = jnp.minimum(1.0, CLIP_NORM / (jnp.sqrt(norm_sq) + 1e-06))
    clipped = clip_factor * mean_grad
    first_new = BETA_ONE * first_moment + (1.0 - BETA_ONE) * clipped
    second_new = BETA_TWO * second_moment + (1.0 - BETA_TWO) * clipped * clipped
    direction = first_new / BIAS_ONE / (jnp.sqrt(second_new / BIAS_TWO) + ADAM_EPS) + DECAY * master
    layer_rate = layer_rates[:, None, None, None]
    master_new = master - layer_rate * direction
    teacher_new = EMA_KEEP * teacher + (1.0 - EMA_KEEP) * master_new
    student_half = master_new.astype(jnp.bfloat16)
    teacher_half = teacher_new.astype(jnp.bfloat16)
    partial_pair = side_by_side((student_half, teacher_half), "fsdp", 2, 0)
    student_weights, teacher_weights = side_by_side((partial_pair[0], partial_pair[1]), DP, 2, 0)
    return (master_new, teacher_new, first_new, second_new, student_weights, teacher_weights)


def solution(mesh):
    torus = Mesh(
        mesh.devices.reshape(4, 2, mesh.shape["fsdp"], mesh.shape["mp"]),
        ("dp_0", "dp_1", "fsdp", "mp"),
    )
    in_specs = (
        P(DP_FSDP, None, None, None, "mp"),
        P(None, None, DP_FSDP, "mp"),
        P(None, None, DP_FSDP, "mp"),
        P(None, None, DP_FSDP, "mp"),
        P(None, None, DP_FSDP, "mp"),
        P(),
    )
    out_specs = (
        P(None, None, DP_FSDP, "mp"),
        P(None, None, DP_FSDP, "mp"),
        P(None, None, DP_FSDP, "mp"),
        P(None, None, DP_FSDP, "mp"),
        P(None, None, None, "mp"),
        P(None, None, None, "mp"),
    )
    return jax.shard_map(
        shards, mesh=torus, in_specs=in_specs, out_specs=out_specs, check_vma=False
    )
```

profile of v0, /device:TPU:1, one launch (start us, length us, event | category | flops | bytes accessed | tf_op | source)
XLA Modules:
  0.0 220.4 jit_solution(2304604764215183388)
XLA Ops:
  7.2 0.0 reduce-scatter.2.cloned.1.call-start
  7.2 5.3 %bitcast_convert_fusion = f32[12,2,256,256]{3,2,1,0:T(8,128)} fusion(bf16[1,12,2,256,256]{4,3,2,1,0:T(8,128)(2,1)} %param.6), kind=kLoop, calls=%fused_computation | loop fusion | flops 1572864 | bytes 9437184 | tf_op jit(solution)/shard_map/convert_element_type | solution.py:47
  12.5 0.0 reduce-scatter.2.cloned.1.call-update
  12.6 0.0 copy-start.3
  12.6 0.0 all-gather.2.cloned.1.call-start
  12.7 48.3 %reduce-scatter.2.cloned.1.call-done = f32[12,2,32,256]{3,2,1,0:T(8,128)} async-done(((f32[12,2,256,256]{3,2,1,0:T(8,128)}), f32[12,2,32,256]{3,2,1,0:T(8,128)}) %reduce-scatter.2.cloned.1.call-update) | async-done | bytes 786448 | tf_op jit(solution)/shard_map/reduce_scatter | solution.py:48
  61.0 1.7 copy.36
  62.7 0.2 copy.37
  62.9 27.6 %all_to_all.5 = f32[8,12,2,4,256]{4,3,2,1,0:T(4,128)S(1)} all-to-all(f32[8,12,2,4,256]{4,3,2,1,0:T(4,128)S(1)} %copy.37), channel_id=1, replica_groups=mesh['dp_0'=4,'dp_1'=2,'fsdp'=8,'mp'=4] {'fsdp'}, dimensions={0} | all-to-all | bytes 1572864 | tf_op jit(solution)/shard_map/all_to_all | solution.py:27
  90.5 0.1 reduce_sum.18
  90.6 0.7 multiply_reduce_fusion
  91.3 11.4 %psum.28 = f32[]{:T(128)} all-reduce(f32[]{:T(128)} %multiply_reduce_fusion), channel_id=1, replica_groups=mesh['dp_0'=4,'dp_1'=2,'fsdp'=8,'mp'=4] {'dp_0'}, use_global_device_ids=true, to_apply=%region_3.0 | all-reduce | flops 1 | bytes 8 | tf_op jit(solution)/shard_map/psum | solution.py:33
  102.7 5.2 %psum.29 = f32[]{:T(128)} all-reduce(f32[]{:T(128)} %psum.28), channel_id=1, replica_groups=mesh['dp_0'=4,'dp_1'=2,'fsdp'=8,'mp'=4] {'dp_1'}, use_global_device_ids=true, to_apply=%region_4.0 | all-reduce | flops 1 | bytes 8 | tf_op jit(solution)/shard_map/psum | solution.py:33
  107.9 11.6 %psum.30 = f32[]{:T(128)} all-reduce(f32[]{:T(128)} %psum.29), channel_id=1, replica_groups=mesh['dp_0'=4,'dp_1'=2,'fsdp'=8,'mp'=4] {'fsdp'}, use_global_device_ids=true, to_apply=%region_5.0 | all-reduce | flops 1 | bytes 8 | tf_op jit(solution)/shard_map/psum | solution.py:33
  119.5 9.0 %psum.31 = f32[]{:T(128)} all-reduce(f32[]{:T(128)} %psum.30), channel_id=1, replica_groups=mesh['dp_0'=4,'dp_1'=2,'fsdp'=8,'mp'=4] {'mp'}, use_global_device_ids=true, to_apply=%region_6.0 | all-reduce | flops 1 | bytes 8 | tf_op jit(solution)/shard_map/psum | solution.py:33
  129.3 0.8 fusion.1
  130.1 0.7 fusion.3
  130.8 0.1 pad_maximum_fusion
  130.9 22.5 %all_gather.6 = bf16[24,2,32,256]{3,0,1,2:T(8,128)(2,1)} all-gather(bf16[24,2,4,256]{3,0,1,2:T(8,128)(2,1)S(1)} %copy.38), channel_id=1, replica_groups=mesh['dp_0'=4,'dp_1'=2,'fsdp'=8,'mp'=4] {'fsdp'}, dimensions={2}, use_global_device_ids=true | all-gather | bytes 884736 | tf_op jit(solution)/shard_map/all_gather | solution.py:43
  153.4 0.0 all-gather.2.cloned.1.call-update
  153.5 48.7 %all-gather.2.cloned.1.call-done = bf16[24,2,256,256]{3,0,1,2:T(8,128)(2,1)} async-done(((bf16[24,2,32,256]{3,0,1,2:T(8,128)(2,1)}), bf16[24,2,256,256]{3,0,1,2:T(8,128)(2,1)}) %all-gather.2.cloned.1.call-update) | async-done | bytes 6291472 | tf_op jit(solution)/shard_map/all_gather | solution.py:43
  202.2 4.5 %fusion.4 = (bf16[12,2,256,256]{3,0,1,2:T(8,128)(2,1)S(1)}, bf16[12,2,256,256]{3,0,1,2:T(8,128)(2,1)S(1)}) fusion(bf16[24,2,256,256]{3,0,1,2:T(8,128)(2,1)} %all-gather.2.cloned.1.call-done), kind=kLoop, calls=%fused_computation.10 | loop fusion | bytes 12582912 | tf_op jit(solution)/shard_map/split | solution.py:43
  206.7 3.5 %copy.40 = bf16[12,2,256,256]{3,2,1,0:T(8,128)(2,1)} copy(bf16[12,2,256,256]{3,0,1,2:T(8,128)(2,1)S(1)} %get-tuple-element.30) | data formatting | bytes 6291456
  210.1 3.5 %copy.39 = bf16[12,2,256,256]{3,2,1,0:T(8,128)(2,1)} copy(bf16[12,2,256,256]{3,0,1,2:T(8,128)(2,1)S(1)} %get-tuple-element.31) | data formatting | bytes 6291456
  (12 shorter events, 0.1 us)
Async XLA Ops:
  7.2 53.8 %reduce-scatter.2.cloned.1.call-start = ((), (), s32[]{:S(2)}) async-start(), calls=%async_computation.2 | async-start | bytes 7077888 | tf_op jit(solution)/shard_map/reduce_scatter | solution.py:48
  12.5 116.7 %copy-start.2 = (f32[12,2,4,256]{3,2,1,0:T(4,128)S(1)}, f32[12,2,4,256]{3,2,1,0:T(4,128)}, u32[]{:S(2)}) copy-start(f32[12,2,4,256]{3,2,1,0:T(4,128)} %param.7) | copy-start | bytes 294916
  12.6 116.7 %copy-start.3 = (f32[12,2,4,256]{3,2,1,0:T(4,128)S(1)}, f32[12,2,4,256]{3,2,1,0:T(4,128)}, u32[]{:S(2)}) copy-start(f32[12,2,4,256]{3,2,1,0:T(4,128)} %param.9) | copy-start | bytes 294916
  12.6 116.7 %copy-start.4 = (f32[12,2,4,256]{3,2,1,0:T(4,128)S(1)}, f32[12,2,4,256]{3,2,1,0:T(4,128)}, u32[]{:S(2)}) copy-start(f32[12,2,4,256]{3,2,1,0:T(4,128)} %param.10) | copy-start | bytes 294916
  12.6 116.7 %copy-start.5 = (f32[12]{0:T(128)S(1)}, f32[12]{0:T(128)}, u32[]{:S(2)}) copy-start(f32[12]{0:T(128)} %param.11) | copy-start | bytes 148
  12.6 117.5 %copy-start.1 = (f32[12,2,4,256]{3,2,1,0:T(4,128)S(1)}, f32[12,2,4,256]{3,2,1,0:T(4,128)}, u32[]{:S(2)}) copy-start(f32[12,2,4,256]{3,2,1,0:T(4,128)} %param.8) | copy-start | bytes 294916
  12.6 189.5 %all-gather.2.cloned.1.call-start = ((), (), s32[]{:S(2)}) async-start(), calls=%async_computation.3 | async-start | bytes 7077888 | tf_op jit(solution)/shard_map/all_gather | solution.py:43
  130.1 76.5 %copy-start = (f32[12,2,4,256]{3,2,1,0:T(4,128)}, f32[12,2,4,256]{3,2,1,0:T(4,128)S(1)}, u32[]{:S(2)}) copy-start(f32[12,2,4,256]{3,2,1,0:T(4,128)S(1)} %get-tuple-element.25) | copy-start | bytes 294916
Sparse Core Ops, SparseCore 0:
  12.7 48.2 reduce-scatter.1
  153.6 48.5 all-gather.1
where the time goes:
time: 221 us; the launch traced here: 220 us
  waiting for transfers between devices  97 us (44%)
  blocking collectives  87.3 us (40%)
  between operations  14.9 us (7%)
  local copies, waits for them, and re-layouts  13.4 us (6%)
  other arithmetic  7.69 us (3%)
    all_gather x1, waiting for transfers between devices, side_by_side(): lax.all_gather(both, axis, axis=dim, tiled=True)  48.7 us
    reduce_scatter x1, waiting for transfers between devices, shards(): halfway = lax.psum_scatter(own_grad, DP, scatter_dimension=2, tiled=True)  48.3 us
    psum x4, blocking collectives, by_axis(): x = lax.psum(x, axis)  37.2 us
    all_to_all x1, blocking collectives, summed_on_arrival(): pieces = lax.all_to_all(cut_along(x, dim, length), axis, 0, 0, tiled=True)  27.6 us
    all_gather x1, blocking collectives, side_by_side(): lax.all_gather(both, axis, axis=dim, tiled=True)  22.5 us
    unnamed x14, local copies, waits for them, and re-layouts  6.99 us
    convert_element_type x1, other arithmetic, shards(): own_grad = gradients[0].astype(jnp.float32)  5.31 us
    split x1, local copies, waits for them, and re-layouts, side_by_side(): jnp.split(lax.all_gather(both, axis, axis=dim, tiled=True), ends, axis=al...  4.48 us
  transfers between devices with their start and end apart: 2, of which 2 were waited for; matrix products, arithmetic and copies ran while one was open for 0% of the time, Pallas kernels for 0%

commit v1 on v0

--- a/solution.py
+++ b/solution.py
@@ -30,7 +30,7 @@
 
 def by_axis(x, axes):
     for axis in axes:
-        x = lax.psum(x, axis)
+        x = jnp.sum(jax.lax.all_gather(x, axis), axis=0)
     return x
 
 

time: 221 us -> 229 us (1.036)
  blocking collectives: 87.3 us -> 54.4 us
  waiting for transfers between devices: 97 us -> 120 us
  local copies, waits for them, and re-layouts: 13.4 us -> 22.3 us
  starting transfers between devices: 0.08 us -> 6.81 us
  other arithmetic: 7.69 us -> 10.1 us
    psum x4 -> x0, blocking collectives: 37.2 us -> none  [by_axis(): x = lax.psum(x, axis)]
    unnamed x0 -> x4, blocking collectives: none -> 32.2 us
    all_to_all x1 -> x0, blocking collectives: 27.6 us -> none  [summed_on_arrival(): pieces = lax.all_to_all(cut_along(x, dim, length), axis, 0, 0, tiled=True)]
    all_to_all x0 -> x1, waiting for transfers between devices: none -> 22.9 us  [summed_on_arrival(): pieces = lax.all_to_all(cut_along(x, dim, length), axis, 0, 0, tiled=True)]
    unnamed x14 -> x34, local copies, waits for them, and re-layouts: 6.99 us -> 15 us
    all_to_all x0 -> x1, starting transfers between devices: none -> 6.73 us  [summed_on_arrival(): pieces = lax.all_to_all(cut_along(x, dim, length), axis, 0, 0, tiled=True)]
    reduce_sum x0 -> x4, other arithmetic: none -> 2.41 us  [by_axis(): x = jnp.sum(jax.lax.all_gather(x, axis), axis=0)]
  transfers between devices with their start and end apart: 2 -> 3, of which waited for: 2 -> 3; matrix products, arithmetic and copies ran while one was open for 0% -> 0% of each run, Pallas kernels for 0% -> 0%
where the time goes in v1:
time: 229 us
  waiting for transfers between devices  120 us (52%)
  blocking collectives  54.4 us (24%)
  local copies, waits for them, and re-layouts  22.3 us (10%)
  between operations  14.9 us (7%)
  other arithmetic  10.1 us (4%)
  starting transfers between devices  6.81 us (3%)
    all_gather x1, waiting for transfers between devices, side_by_side(): lax.all_gather(both, axis, axis=dim, tiled=True)  48.9 us
    reduce_scatter x1, waiting for transfers between devices, shards(): halfway = lax.psum_scatter(own_grad, DP, scatter_dimension=2, tiled=True)  48.3 us
    unnamed x4, blocking collectives  32.2 us
    all_to_all x1, waiting for transfers between devices, summed_on_arrival(): pieces = lax.all_to_all(cut_along(x, dim, length), axis, 0, 0, tiled=True)  22.9 us
    all_gather x1, blocking collectives, side_by_side(): lax.all_gather(both, axis, axis=dim, tiled=True)  22.2 us
    unnamed x34, local copies, waits for them, and re-layouts  15 us
    all_to_all x1, starting transfers between devices, summed_on_arrival(): pieces = lax.all_to_all(cut_along(x, dim, length), axis, 0, 0, tiled=True)  6.73 us
    convert_element_type x1, other arithmetic, shards(): own_grad = gradients[0].astype(jnp.float32)  5.31 us
  transfers between devices with their start and end apart: 3, of which 3 were waited for; matrix products, arithmetic and copies ran while one was open for 0% of the time, Pallas kernels for 0%

profile of v1, /device:TPU:1, one launch (start us, length us, event | category | flops | bytes accessed | tf_op | source)
XLA Modules:
  0.0 228.7 jit_solution(6026501045474592375)
XLA Ops:
  7.2 5.3 %bitcast_convert_fusion = f32[12,2,256,256]{3,2,1,0:T(8,128)} fusion(bf16[1,12,2,256,256]{4,3,2,1,0:T(8,128)(2,1)} %param.6), kind=kLoop, calls=%fused_computation | loop fusion | flops 1572864 | bytes 9437184 | tf_op jit(solution)/shard_map/convert_element_type | solution.py:47
  12.6 48.3 %reduce-scatter.2.cloned.1.call-done = f32[12,2,32,256]{3,2,1,0:T(8,128)} async-done(((f32[12,2,256,256]{3,2,1,0:T(8,128)}), f32[12,2,32,256]{3,2,1,0:T(8,128)}) %reduce-scatter.2.cloned.1.call-update) | async-done | bytes 786448 | tf_op jit(solution)/shard_map/reduce_scatter | solution.py:48
  61.0 1.7 copy.36
  62.7 1.1 copy.37
  63.8 6.7 %all-to-all-start = ((f32[8,12,2,4,256]{4,3,2,1,0:T(4,128)}), f32[8,12,2,4,256]{4,3,2,1,0:T(4,128)S(1)}, u32[]{:S(2)}, u32[]{:S(2)}) async-start(f32[8,12,2,4,256]{4,3,2,1,0:T(4,128)} %copy.37), calls=%async_computation.1 | async-start | bytes 1572864 | tf_op jit(solution)/shard_map/all_to_all | solution.py:27
  71.2 22.9 %all-to-all-done = f32[8,12,2,4,256]{4,3,2,1,0:T(4,128)S(1)} async-done(((f32[8,12,2,4,256]{4,3,2,1,0:T(4,128)}), f32[8,12,2,4,256]{4,3,2,1,0:T(4,128)S(1)}, u32[]{:S(2)}, u32[]{:S(2)}) %all-to-all-start) | async-done | bytes 786464 | tf_op jit(solution)/shard_map/all_to_all | solution.py:27
  94.3 0.7 multiply_reduce_fusion
  94.9 1.4 dynamic-update-slice
  96.9 8.3 %all-reduce = f32[4]{0:T(128)S(1)} all-reduce(f32[4]{0:T(128)S(1)} %dynamic-update-slice), channel_id=1, replica_groups=mesh['dp_0'=4,'dp_1'=2,'fsdp'=8,'mp'=4] {'dp_0'}, use_global_device_ids=true, to_apply=%add | all-reduce | flops 4 | bytes 32
  105.2 0.6 reduce_sum.56
  105.8 1.4 dynamic-update-slice.1
  107.8 4.6 %all-reduce.1 = f32[2]{0:T(128)S(1)} all-reduce(f32[2]{0:T(128)S(1)} %dynamic-update-slice.1), channel_id=1, replica_groups=mesh['dp_0'=4,'dp_1'=2,'fsdp'=8,'mp'=4] {'dp_1'}, use_global_device_ids=true, to_apply=%add.1 | all-reduce | flops 2 | bytes 16
  113.0 1.4 dynamic-update-slice.2
  115.0 10.8 %all-reduce.2 = f32[8]{0:T(128)S(1)} all-reduce(f32[8]{0:T(128)S(1)} %dynamic-update-slice.2), channel_id=1, replica_groups=mesh['dp_0'=4,'dp_1'=2,'fsdp'=8,'mp'=4] {'fsdp'}, use_global_device_ids=true, to_apply=%add.2 | all-reduce | flops 8 | bytes 64
  125.8 0.6 reduce_sum.58
  126.4 1.4 dynamic-update-slice.3
  127.8 8.4 %all-reduce.3 = f32[4]{0:T(128)S(1)} all-reduce(f32[4]{0:T(128)S(1)} %dynamic-update-slice.3), channel_id=1, replica_groups=mesh['dp_0'=4,'dp_1'=2,'fsdp'=8,'mp'=4] {'mp'}, use_global_device_ids=true, to_apply=%add.3 | all-reduce | flops 4 | bytes 32
  137.6 0.8 fusion.1
  138.5 0.7 fusion.3
  139.3 22.2 %all_gather.38 = bf16[24,2,32,256]{3,0,1,2:T(8,128)(2,1)} all-gather(bf16[24,2,4,256]{3,0,1,2:T(8,128)(2,1)S(1)} %copy.38), channel_id=1, replica_groups=mesh['dp_0'=4,'dp_1'=2,'fsdp'=8,'mp'=4] {'fsdp'}, dimensions={2}, use_global_device_ids=true | all-gather | bytes 884736 | tf_op jit(solution)/shard_map/all_gather | solution.py:43
  161.5 48.9 %all-gather.2.cloned.1.call-done = bf16[24,2,256,256]{3,0,1,2:T(8,128)(2,1)} async-done(((bf16[24,2,32,256]{3,0,1,2:T(8,128)(2,1)}), bf16[24,2,256,256]{3,0,1,2:T(8,128)(2,1)}) %all-gather.2.cloned.1.call-update) | async-done | bytes 6291472 | tf_op jit(solution)/shard_map/all_gather | solution.py:43
  210.4 4.5 %fusion.4 = (bf16[12,2,256,256]{3,0,1,2:T(8,128)(2,1)S(1)}, bf16[12,2,256,256]{3,0,1,2:T(8,128)(2,1)S(1)}) fusion(bf16[24,2,256,256]{3,0,1,2:T(8,128)(2,1)} %all-gather.2.cloned.1.call-done), kind=kLoop, calls=%fused_computation.10 | loop fusion | bytes 12582912 | tf_op jit(solution)/shard_map/split | solution.py:43
  214.9 3.5 %copy.40 = bf16[12,2,256,256]{3,2,1,0:T(8,128)(2,1)} copy(bf16[12,2,256,256]{3,0,1,2:T(8,128)(2,1)S(1)} %get-tuple-element.30) | data formatting | bytes 6291456
  218.4 3.5 %copy.39 = bf16[12,2,256,256]{3,2,1,0:T(8,128)(2,1)} copy(bf16[12,2,256,256]{3,0,1,2:T(8,128)(2,1)S(1)} %get-tuple-element.31) | data formatting | bytes 6291456
  (37 shorter events, 3.9 us)
Async XLA Ops:
  7.2 53.8 %reduce-scatter.2.cloned.1.call-start = ((), (), s32[]{:S(2)}) async-start(), calls=%async_computation.2 | async-start | bytes 7077888 | tf_op jit(solution)/shard_map/reduce_scatter | solution.py:48
  12.5 58.1 %copy-start.9 = (u32[256]{0:T(256)S(1)}, u32[256]{0:T(256)}, u32[]{:S(2)}) copy-start(u32[256]{0:T(256)} %constant.37) | copy-start | bytes 3076
  12.6 83.8 %copy-start.8 = (u32[256]{0:T(256)S(1)}, u32[256]{0:T(256)}, u32[]{:S(2)}) copy-start(u32[256]{0:T(256)} %constant.42) | copy-start | bytes 3076
  12.6 94.6 %copy-start.7 = (u32[256]{0:T(256)S(1)}, u32[256]{0:T(256)}, u32[]{:S(2)}) copy-start(u32[256]{0:T(256)} %constant.47) | copy-start | bytes 3076
  12.6 101.8 %copy-start.6 = (u32[256]{0:T(256)S(1)}, u32[256]{0:T(256)}, u32[]{:S(2)}) copy-start(u32[256]{0:T(256)} %constant.52) | copy-start | bytes 3076
  12.6 125.0 %copy-start.2 = (f32[12,2,4,256]{3,2,1,0:T(4,128)S(1)}, f32[12,2,4,256]{3,2,1,0:T(4,128)}, u32[]{:S(2)}) copy-start(f32[12,2,4,256]{3,2,1,0:T(4,128)} %param.7) | copy-start | bytes 294916
  12.6 125.0 %copy-start.3 = (f32[12,2,4,256]{3,2,1,0:T(4,128)S(1)}, f32[12,2,4,256]{3,2,1,0:T(4,128)}, u32[]{:S(2)}) copy-start(f32[12,2,4,256]{3,2,1,0:T(4,128)} %param.9) | copy-start | bytes 294916
  12.6 125.0 %copy-start.4 = (f32[12,2,4,256]{3,2,1,0:T(4,128)S(1)}, f32[12,2,4,256]{3,2,1,0:T(4,128)}, u32[]{:S(2)}) copy-start(f32[12,2,4,256]{3,2,1,0:T(4,128)} %param.10) | copy-start | bytes 294916
  12.6 125.0 %copy-start.5 = (f32[12]{0:T(128)S(1)}, f32[12]{0:T(128)}, u32[]{:S(2)}) copy-start(f32[12]{0:T(128)} %param.11) | copy-start | bytes 148
  12.6 125.8 %copy-start.1 = (f32[12,2,4,256]{3,2,1,0:T(4,128)S(1)}, f32[12,2,4,256]{3,2,1,0:T(4,128)}, u32[]{:S(2)}) copy-start(f32[12,2,4,256]{3,2,1,0:T(4,128)} %param.8) | copy-start | bytes 294916
  63.8 30.3 %all-to-all-start = ((f32[8,12,2,4,256]{4,3,2,1,0:T(4,128)}), f32[8,12,2,4,256]{4,3,2,1,0:T(4,128)S(1)}, u32[]{:S(2)}, u32[]{:S(2)}) async-start(f32[8,12,2,4,256]{4,3,2,1,0:T(4,128)} %copy.37), calls=%async_computation.1 | async-start | bytes 1572864 | tf_op jit(solution)/shard_map/all_to_all | solution.py:27
  70.5 139.8 %all-gather.2.cloned.1.call-start = ((), (), s32[]{:S(2)}) async-start(), calls=%async_computation.3 | async-start | bytes 7077888 | tf_op jit(solution)/shard_map/all_gather | solution.py:43
  138.5 76.4 %copy-start = (f32[12,2,4,256]{3,2,1,0:T(4,128)}, f32[12,2,4,256]{3,2,1,0:T(4,128)S(1)}, u32[]{:S(2)}) copy-start(f32[12,2,4,256]{3,2,1,0:T(4,128)S(1)} %get-tuple-element.25) | copy-start | bytes 294916
Sparse Core Ops, SparseCore 0:
  12.7 48.2 reduce-scatter.1
  161.6 48.6 all-gather.1
